TPU v7x, 256 devices: a whole 4x4x8 slice. The times are simulated.
256 devices in a mesh: replica: 64 (over z, y, core), model: 4 (over x).
Axes of the slice: x: 4, y: 4, z: 8, core: 2. Of those that a mesh axis runs over, the one named last changes fastest.
Arguments:
- partial_up: float32 [64, 1024, 4096], P('replica', None, 'model'), may hold values from -8 to 8
- partial_down: float32 [64, 4096, 1024], P('replica', 'model'), may hold values from -8 to 8
- partial_norm: float32 [64, 1024], P('replica'), may hold values from -16 to 16
- partial_bias: float32 [64, 1024], P('replica'), may hold values from -16 to 16
- master_up: float32 [1024, 4096], P('replica', 'model'), may hold values from -0.1875 to 0.1875
- master_down: float32 [4096, 1024], P('model', 'replica'), may hold values from -0.09375 to 0.09375
- master_norm: float32 [1024], P('replica'), may hold values from 0.25 to 1.75
- master_bias: float32 [1024], P('replica'), may hold values from -3 to 3
- memory_up: float32 [1024, 4096], P('replica', 'model'), may hold values from 0.05 to 0.8
- memory_down: float32 [4096, 1024], P('model', 'replica'), may hold values from 0.05 to 0.8
- memory_norm: float32 [1024], P('replica'), may hold values from 0.05 to 0.8
- memory_bias: float32 [1024], P('replica'), may hold values from 0.05 to 0.8
Outputs:
- compute_up: bfloat16 [1024, 4096], P(None, 'model')
- compute_down: bfloat16 [4096, 1024], P('model')
- compute_norm: bfloat16 [1024], replicated
- compute_bias: bfloat16 [1024], replicated
- stepped_up: float32 [1024, 4096], P('replica', 'model')
- stepped_down: float32 [4096, 1024], P('model', 'replica')
- stepped_norm: float32 [1024], P('replica')
- stepped_bias: float32 [1024], P('replica')
- state_new_up: float32 [1024, 4096], P('replica', 'model')
- state_new_down: float32 [4096, 1024], P('model', 'replica')
- state_new_norm: float32 [1024], P('replica')
- state_new_bias: float32 [1024], P('replica')
All inputs are finite; a program needn't handle non-finite values.
Results may differ from a plain program's by a relative error of at most 0.001.
Values may be sent and summed in bfloat16 or wider, within the bound.
A program may use at most 128 MiB of HBM per device.

v0:
```python
import jax
import jax.numpy as jnp
from jax import lax
from jax.sharding import PartitionSpec as P

learn_rate = 0.05
hold_rate = 0.9


def in_blocks(shard, dim, size):
    before, after = (shard.shape[:dim], shard.shape[dim + 1 :])
    return jnp.moveaxis(shard.reshape(*before, size, -1, *after), dim, 0)


def sum_packed(arrays, axis, dims):
    size = lax.axis_size(axis)
    tiles = [in_blocks(a, dim, size) for a, dim in zip(arrays, dims)]
    lines = jnp.concatenate([b.reshape(size, -1) for b in tiles], axis=1)
    width = max(16, -(-lines.shape[1] // 1024) * 8)
    lines = jnp.pad(lines, ((0, 0), (0, width * 128 - lines.shape[1]))).reshape(-1, 128)
    line, at, done = (lax.psum_scatter(lines, axis, tiled=True).reshape(-1), 0, [])
    for b in tiles:
        part = b[0]
        done.append(line[at : at + part.size].reshape(part.shape))
        at += part.size
    return tuple(done)


def from_everyone(shard, axis):
    size = lax.axis_size(axis)
    return lax.all_to_all(
        jnp.broadcast_to(shard[None], (size, *shard.shape)), axis, 0, 0, tiled=True
    )


def over_copies(shard, axis):
    everything = from_everyone(shard, axis)
    return jnp.sum(everything, axis=0)


def packed_total(arrays, axis):
    ends = [0]
    for a in arrays:
        ends.append(ends[-1] + a.size)
    total = over_copies(jnp.concatenate([a.ravel() for a in arrays]), axis)
    return tuple((total[b:e].reshape(a.shape) for a, b, e in zip(arrays, ends, ends[1:])))


def gather_turned(arrays, axis, dims):
    turned = [jnp.moveaxis(a, dim, 0) for a, dim in zip(arrays, dims)]
    both = jnp.concatenate([t.reshape(len(t), -1) for t in turned], axis=1)
    out, at, done = (lax.all_gather(both, axis, axis=0, tiled=True), 0, [])
    for t, dim in zip(turned, dims):
        section = out[:, at : at + t[0].size].reshape(-1, *t.shape[1:])
        done.append(jnp.moveaxis(section, 0, dim))
        at += t[0].size
    return tuple(done)


def on_device(
    partial_up,
    partial_down,
    partial_norm,
    partial_bias,
    master_up,
    master_down,
    master_norm,
    master_bias,
    memory_up,
    memory_down,
    memory_norm,
    memory_bias,
):
    mean_up, mean_down = sum_packed((partial_up[0], partial_down[0]), "replica", (0, 1))
    whole_norm, whole_bias = packed_total((partial_norm[0], partial_bias[0]), "replica")
    place = lax.axis_index("replica")
    mean_norm = lax.dynamic_slice_in_dim(
        whole_norm, place * master_norm.shape[0], master_norm.shape[0]
    )
    mean_bias = lax.dynamic_slice_in_dim(
        whole_bias, place * master_bias.shape[0], master_bias.shape[0]
    )
    mean_rate = lax.axis_size("replica") ** (-0.5)
    mean_up = mean_up * mean_rate
    mean_down = mean_down * mean_rate
    mean_norm = mean_norm * mean_rate
    mean_bias = mean_bias * mean_rate
    state_new_up = hold_rate * memory_up + (1.0 - hold_rate) * mean_up * mean_up
    stepped_up = master_up - learn_rate * mean_up * lax.rsqrt(state_new_up + 1e-06)
    state_new_down = hold_rate * memory_down + (1.0 - hold_rate) * mean_down * mean_down
    stepped_down = master_down - learn_rate * mean_down * lax.rsqrt(state_new_down + 1e-06)
    state_new_norm = hold_rate * memory_norm + (1.0 - hold_rate) * mean_norm * mean_norm
    stepped_norm = master_norm - learn_rate * mean_norm * lax.rsqrt(state_new_norm + 1e-06)
    state_new_bias = hold_rate * memory_bias + (1.0 - hold_rate) * mean_bias * mean_bias
    stepped_bias = master_bias - learn_rate * mean_bias * lax.rsqrt(state_new_bias + 1e-06)
    compute_up, compute_down, compute_norm, compute_bias = gather_turned(
        (
            stepped_up.astype(jnp.bfloat16),
            stepped_down.astype(jnp.bfloat16),
            stepped_norm.astype(jnp.bfloat16),
            stepped_bias.astype(jnp.bfloat16),
        ),
        "replica",
        (0, 1, 0, 0),
    )
    return (
        compute_up,
        compute_down,
        compute_norm,
        compute_bias,
        stepped_up,
        stepped_down,
        stepped_norm,
        stepped_bias,
        state_new_up,
        state_new_down,
        state_new_norm,
        state_new_bias,
    )


def solution(mesh):
    in_specs = (
        P("replica", None, "model"),
        P("replica", "model", None),
        P("replica", None),
        P("replica", None),
        P("replica", "model"),
        P("model", "replica"),
        P("replica"),
        P("replica"),
        P("replica", "model"),
        P("model", "replica"),
        P("replica"),
        P("replica"),
    )
    out_specs = (
        P(None, "model"),
        P("model", None),
        P(),
        P(),
        P("replica", "model"),
        P("model", "replica"),
        P("replica"),
        P("replica"),
        P("replica", "model"),
        P("model", "replica"),
        P("replica"),
        P("replica"),
    )
    return jax.shard_map(
        on_device, mesh=mesh, in_specs=in_specs, out_specs=out_specs, check_vma=False
    )
```

profile of v0, /device:TPU:1, one launch (start us, length us, event | category | flops | bytes accessed | tf_op | source)
XLA Modules:
  0.0 303.0 jit_solution(8466722291256023141)
XLA Ops:
  7.2 0.0 reduce-scatter.2.cloned.1.call-start
  7.2 5.4 %copy.56 = f32[1,1024,1024]{1,2,0:T(8,128)} copy(f32[1,1024,1024]{2,1,0:T(8,128)} %param.13) | data formatting | bytes 8388608 | tf_op args[1]
  12.6 8.7 %copy.57 = f32[64,1024,16]{0,2,1:T(8,128)} copy(f32[64,1024,16]{1,2,0:T(8,128)} %bitcast.15) | data formatting | bytes 8388608 | tf_op jit(solution)/shard_map/transpose | solution.py:12
  21.3 6.8 %copy.58 = f32[64,16384]{1,0:T(8,128)} copy(f32[64,16384]{0,1:T(8,128)} %bitcast.14) | data formatting | bytes 8388608 | tf_op jit(solution)/shard_map/reshape | solution.py:18
  28.1 4.9 %reshape_reshape_squeeze.3 = f32[64,16384]{1,0:T(8,128)} reshape(f32[1,1024,1024]{2,1,0:T(8,128)} %param.12) | data formatting | bytes 8388608 | tf_op jit(solution)/shard_map/reshape;reshape;squeeze | solution.py:18
  33.0 7.3 %pad_maximum_fusion = f32[64,32768]{1,0:T(8,128)} fusion(f32[64,16384]{1,0:T(8,128)} %copy.58, f32[64,16384]{1,0:T(8,128)} %reshape_reshape_squeeze.3), kind=kLoop, calls=%fused_computation | loop fusion | flops 2097152 | bytes 16777216 | tf_op jit(solution)/shard_map/concatenate | solution.py:18
  40.3 9.3 %reshape.70 = f32[16384,128]{1,0:T(8,128)} reshape(f32[64,32768]{1,0:T(8,128)} %pad_maximum_fusion) | data formatting | bytes 16777216 | tf_op jit(solution)/shard_map/reshape | solution.py:20
  49.6 0.0 copy-start.4
  49.6 0.0 copy-start.5
  49.6 0.0 copy-start.6
  49.6 0.0 copy-start.7
  49.6 0.0 copy-start.8
  49.6 0.0 copy-start.9
  49.6 0.0 reduce-scatter.2.cloned.1.call-update
  49.7 0.0 copy-start
  49.7 0.0 copy-start.1
  49.7 0.0 copy-start.2
  49.7 0.0 copy-start.3
  49.7 0.6 copy-done.4
  50.3 0.0 copy-done.5
  50.3 1.1 broadcast_in_dim.2
  51.4 13.1 %all-to-all-start = ((f32[64,1,2048]{2,1,0:T(1,128)}), f32[64,1,2048]{2,1,0:T(1,128)S(1)}, u32[]{:S(2)}, u32[]{:S(2)}) async-start(f32[64,1,2048]{2,1,0:T(1,128)} %broadcast_in_dim.2), calls=%async_computation.1 | async-start | bytes 1048576 | tf_op jit(solution)/shard_map/all_to_all | solution.py:31
  64.5 0.0 all-gather.2.cloned.1.call-start
  64.6 17.6 %all-to-all-done = f32[64,1,2048]{2,1,0:T(1,128)S(1)} async-done(((f32[64,1,2048]{2,1,0:T(1,128)}), f32[64,1,2048]{2,1,0:T(1,128)S(1)}, u32[]{:S(2)}, u32[]{:S(2)}) %all-to-all-start) | async-done | bytes 524320 | tf_op jit(solution)/shard_map/all_to_all | solution.py:31
  82.2 0.3 reduce_sum.9
  82.5 0.0 copy-done.6
  82.5 0.0 copy-done.7
  82.6 0.0 copy-done.8
  82.6 0.0 copy-done.9
  82.6 0.6 convert_bitcast_fusion.1
  83.2 0.1 copy.62
  83.3 0.1 copy.63
  83.4 117.8 %reduce-scatter.2.cloned.1.call-done = f32[256,128]{1,0:T(8,128)} async-done(((f32[16384,128]{1,0:T(8,128)}), f32[256,128]{1,0:T(8,128)}) %reduce-scatter.2.cloned.1.call-update) | async-done | bytes 131088 | tf_op jit(solution)/shard_map/reduce_scatter | solution.py:21
  201.2 0.9 multiply_multiply_fusion
  202.1 0.2 mul.127
  202.3 0.2 copy.60
  202.5 0.2 mul.133
  202.7 0.2 copy.59
  202.8 0.0 copy-done
  202.8 0.0 copy-done.1
  202.8 0.7 fusion
  203.5 0.0 copy-done.2
  203.5 0.0 copy-done.3
  203.5 0.7 convert_bitcast_fusion
  204.2 0.7 concatenate.11
  204.9 0.0 all-gather.2.cloned.1.call-update
  204.9 82.8 %all-gather.2.cloned.1.call-done = bf16[1024,2050]{1,0:T(8,128)(2,1)} async-done(((bf16[16,2050]{1,0:T(8,128)(2,1)}), bf16[1024,2050]{1,0:T(8,128)(2,1)}) %all-gather.2.cloned.1.call-update) | async-done | bytes 4198416 | tf_op jit(solution)/shard_map/all_gather | solution.py:52
  287.7 4.0 %slice_bitcast_fusion = (bf16[1024,1024]{0,1:T(8,128)(2,1)S(1)}, bf16[1024,1024]{1,0:T(8,128)(2,1)}) fusion(bf16[1024,2050]{1,0:T(8,128)(2,1)} %all-gather.2.cloned.1.call-done), kind=kLoop, calls=%fused_computation.1 | loop fusion | bytes 8388608 | tf_op jit(solution)/shard_map/transpose | solution.py:55
  291.7 2.5 copy.64
  294.2 2.0 slice_reduce_fusion
  (4 shorter events, 0.0 us)
Async XLA Ops:
  7.2 194.0 %reduce-scatter.2.cloned.1.call-start = ((), (), s32[]{:S(2)}) async-start(), calls=%async_computation.2 | async-start | bytes 8519680 | tf_op jit(solution)/shard_map/reduce_scatter | solution.py:21
  49.6 0.7 copy-start.4
  49.6 0.7 copy-start.5
  49.6 32.9 %copy-start.6 = (f32[16]{0:T(128)S(1)}, f32[16]{0:T(128)}, u32[]{:S(2)}) copy-start(f32[16]{0:T(128)} %param.19) | copy-start | bytes 196
  49.6 32.9 %copy-start.7 = (f32[16]{0:T(128)S(1)}, f32[16]{0:T(128)}, u32[]{:S(2)}) copy-start(f32[16]{0:T(128)} %param.23) | copy-start | bytes 196
  49.6 32.9 %copy-start.8 = (f32[16]{0:T(128)S(1)}, f32[16]{0:T(128)}, u32[]{:S(2)}) copy-start(f32[16]{0:T(128)} %param.18) | copy-start | bytes 196
  49.6 32.9 %copy-start.9 = (f32[16]{0:T(128)S(1)}, f32[16]{0:T(128)}, u32[]{:S(2)}) copy-start(f32[16]{0:T(128)} %param.22) | copy-start | bytes 196
  49.7 153.2 %copy-start = (f32[16,1024]{1,0:T(8,128)S(1)}, f32[16,1024]{1,0:T(8,128)}, u32[]{:S(2)}) copy-start(f32[16,1024]{1,0:T(8,128)} %param.16) | copy-start | bytes 196612
  49.7 153.2 %copy-start.1 = (f32[16,1024]{1,0:T(8,128)S(1)}, f32[16,1024]{1,0:T(8,128)}, u32[]{:S(2)}) copy-start(f32[16,1024]{1,0:T(8,128)} %param.20) | copy-start | bytes 196612
  49.7 153.8 %copy-start.2 = (f32[1024,16]{0,1:T(8,128)S(1)}, f32[1024,16]{0,1:T(8,128)}, u32[]{:S(2)}) copy-start(f32[1024,16]{0,1:T(8,128)} %param.17) | copy-start | bytes 196612
  49.7 153.8 %copy-start.3 = (f32[1024,16]{0,1:T(8,128)S(1)}, f32[1024,16]{0,1:T(8,128)}, u32[]{:S(2)}) copy-start(f32[1024,16]{0,1:T(8,128)} %param.21) | copy-start | bytes 196612
  51.4 30.8 %all-to-all-start = ((f32[64,1,2048]{2,1,0:T(1,128)}), f32[64,1,2048]{2,1,0:T(1,128)S(1)}, u32[]{:S(2)}, u32[]{:S(2)}) async-start(f32[64,1,2048]{2,1,0:T(1,128)} %broadcast_in_dim.2), calls=%async_computation.1 | async-start | bytes 1048576 | tf_op jit(solution)/shard_map/all_to_all | solution.py:31
  64.5 223.2 %all-gather.2.cloned.1.call-start = ((), (), s32[]{:S(2)}) async-start(), calls=%async_computation.3 | async-start | bytes 4526080 | tf_op jit(solution)/shard_map/all_gather | solution.py:52
Sparse Core Ops, SparseCore 0:
  49.8 151.3 reduce-scatter.1
  205.1 82.5 all-gather.1
where the time goes:
time: 304 us; the launch traced here: 303 us
  waiting for transfers between devices  218 us (72%)
  local copies, waits for them, and re-layouts  46.9 us (15%)
  between operations  14.2 us (5%)
  starting transfers between devices  13.2 us (4%)
  other arithmetic  10.5 us (3%)
    reduce_scatter x1, waiting for transfers between devices, sum_packed(): lax.psum_scatter(lines, axis, tiled=True).reshape(-1)  118 us
    all_gather x1, waiting for transfers between devices, gather_turned(): out, at, done = (lax.all_gather(both, axis, axis=0, tiled=True), 0, [])  82.8 us
    all_to_all x1, waiting for transfers between devices, from_everyone(): lax.all_to_all(jnp.broadcast_to(shard[None], (size, *shard.shape)), axis,...  17.6 us
    all_to_all x1, starting transfers between devices, from_everyone(): lax.all_to_all(jnp.broadcast_to(shard[None], (size, *shard.shape)), axis,...  13.1 us
    reshape x1, local copies, waits for them, and re-layouts, sum_packed(): jnp.pad(lines, ((0, 0), (0, width * 128 - lines.shape[1]))).reshape(-1, 128)  9.25 us
    transpose x1, local copies, waits for them, and re-layouts, in_blocks(): return jnp.moveaxis(shard.reshape(*before, size, -1, *after), dim, 0)  8.7 us
    unnamed x22, local copies, waits for them, and re-layouts  8.56 us
    concatenate x1, other arithmetic, sum_packed(): lines = jnp.concatenate([b.reshape(size, -1) for b in tiles], axis=1)  7.3 us
  transfers between devices with their start and end apart: 3, of which 3 were waited for; matrix products, arithmetic and copies ran while one was open for 1% of the time, Pallas kernels for 0%

commit v1 on v0

--- a/solution.py
+++ b/solution.py
@@ -49,7 +49,13 @@
 def gather_turned(arrays, axis, dims):
     turned = [jnp.moveaxis(a, dim, 0) for a, dim in zip(arrays, dims)]
     both = jnp.concatenate([t.reshape(len(t), -1) for t in turned], axis=1)
-    out, at, done = (lax.all_gather(both, axis, axis=0, tiled=True), 0, [])
+    out, at, done = (
+        jnp.concatenate(
+            lax.all_to_all(jnp.stack([both] * lax.axis_size(axis)), axis, 0, 0), axis=0
+        ),
+        0,
+        [],
+    )
     for t, dim in zip(turned, dims):
         section = out[:, at : at + t[0].size].reshape(-1, *t.shape[1:])
         done.append(jnp.moveaxis(section, 0, dim))

time: 304 us -> 333 us (1.095)
  blocking collectives: 0 us -> 115 us
  waiting for transfers between devices: 218 us -> 136 us
  local copies, waits for them, and re-layouts: 46.9 us -> 43.5 us
    all_to_all x0 -> x1, blocking collectives: none -> 115 us  [gather_turned(): lax.all_to_all(jnp.stack([both] * lax.axis_size(axis)), axis, 0, 0)]
    all_gather x1 -> x0, waiting for transfers between devices: 82.8 us -> none  [gather_turned(): out, at, done = (lax.all_gather(both, axis, axis=0, tiled=True), 0, [])]
  transfers between devices with their start and end apart: 3 -> 2, of which waited for: 3 -> 2; matrix products, arithmetic and copies ran while one was open for 1% -> 1% of each run, Pallas kernels for 0% -> 0%
where the time goes in v1:
time: 333 us; the launch traced here: 332 us
  waiting for transfers between devices  136 us (41%)
  blocking collectives  115 us (35%)
  local copies, waits for them, and re-layouts  43.5 us (13%)
  between operations  14.2 us (4%)
  starting transfers between devices  13.2 us (4%)
  other arithmetic  10.5 us (3%)
    reduce_scatter x1, waiting for transfers between devices, sum_packed(): lax.psum_scatter(lines, axis, tiled=True).reshape(-1)  118 us
    all_to_all x1, blocking collectives, gather_turned(): lax.all_to_all(jnp.stack([both] * lax.axis_size(axis)), axis, 0, 0)  115 us
    all_to_all x1, waiting for transfers between devices, from_everyone(): lax.all_to_all(jnp.broadcast_to(shard[None], (size, *shard.shape)), axis,...  17.7 us
    all_to_all x1, starting transfers between devices, from_everyone(): lax.all_to_all(jnp.broadcast_to(shard[None], (size, *shard.shape)), axis,...  13.1 us
    reshape x1, local copies, waits for them, and re-layouts, sum_packed(): jnp.pad(lines, ((0, 0), (0, width * 128 - lines.shape[1]))).reshape(-1, 128)  9.25 us
    transpose x1, local copies, waits for them, and re-layouts, in_blocks(): return jnp.moveaxis(shard.reshape(*before, size, -1, *after), dim, 0)  8.7 us
    unnamed x22, local copies, waits for them, and re-layouts  8.56 us
    concatenate x1, other arithmetic, sum_packed(): lines = jnp.concatenate([b.reshape(size, -1) for b in tiles], axis=1)  7.29 us
  transfers between devices with their start and end apart: 2, of which 2 were waited for; matrix products, arithmetic and copies ran while one was open for 1% of the time, Pallas kernels for 0%

profile of v1, /device:TPU:1, one launch (start us, length us, event | category | flops | bytes accessed | tf_op | source)
XLA Modules:
  0.0 332.2 jit_solution(8138375754436686522)
XLA Ops:
  7.2 0.0 reduce-scatter.2.cloned.1.call-start
  7.2 5.4 %copy.58 = f32[1,1024,1024]{1,2,0:T(8,128)} copy(f32[1,1024,1024]{2,1,0:T(8,128)} %param.13) | data formatting | bytes 8388608 | tf_op args[1]
  12.6 8.7 %copy.59 = f32[64,1024,16]{0,2,1:T(8,128)} copy(f32[64,1024,16]{1,2,0:T(8,128)} %bitcast.18) | data formatting | bytes 8388608 | tf_op jit(solution)/shard_map/transpose | solution.py:12
  21.3 6.8 %copy.60 = f32[64,16384]{1,0:T(8,128)} copy(f32[64,16384]{0,1:T(8,128)} %bitcast.15) | data formatting | bytes 8388608 | tf_op jit(solution)/shard_map/reshape | solution.py:18
  28.1 4.9 %reshape_reshape_squeeze.3 = f32[64,16384]{1,0:T(8,128)} reshape(f32[1,1024,1024]{2,1,0:T(8,128)} %param.12) | data formatting | bytes 8388608 | tf_op jit(solution)/shard_map/reshape;reshape;squeeze | solution.py:18
  33.1 7.3 %pad_maximum_fusion = f32[64,32768]{1,0:T(8,128)} fusion(f32[64,16384]{1,0:T(8,128)} %copy.60, f32[64,16384]{1,0:T(8,128)} %reshape_reshape_squeeze.3), kind=kLoop, calls=%fused_computation | loop fusion | flops 2097152 | bytes 16777216 | tf_op jit(solution)/shard_map/concatenate | solution.py:18
  40.4 9.3 %reshape.75 = f32[16384,128]{1,0:T(8,128)} reshape(f32[64,32768]{1,0:T(8,128)} %pad_maximum_fusion) | data formatting | bytes 16777216 | tf_op jit(solution)/shard_map/reshape | solution.py:20
  49.6 0.0 copy-start.4
  49.6 0.0 copy-start.5
  49.6 0.0 copy-start.6
  49.6 0.0 copy-start.7
  49.6 0.0 copy-start.8
  49.6 0.0 copy-start.9
  49.6 0.0 reduce-scatter.2.cloned.1.call-update
  49.7 0.0 copy-start
  49.7 0.0 copy-start.1
  49.7 0.0 copy-start.2
  49.7 0.0 copy-start.3
  49.7 0.6 copy-done.4
  50.3 0.0 copy-done.5
  50.3 1.1 broadcast_in_dim.2
  51.4 13.1 %all-to-all-start = ((f32[64,1,2048]{2,1,0:T(1,128)}), f32[64,1,2048]{2,1,0:T(1,128)S(1)}, u32[]{:S(2)}, u32[]{:S(2)}) async-start(f32[64,1,2048]{2,1,0:T(1,128)} %broadcast_in_dim.2), calls=%async_computation.1 | async-start | bytes 1048576 | tf_op jit(solution)/shard_map/all_to_all | solution.py:31
  64.5 17.7 %all-to-all-done = f32[64,1,2048]{2,1,0:T(1,128)S(1)} async-done(((f32[64,1,2048]{2,1,0:T(1,128)}), f32[64,1,2048]{2,1,0:T(1,128)S(1)}, u32[]{:S(2)}, u32[]{:S(2)}) %all-to-all-start) | async-done | bytes 524320 | tf_op jit(solution)/shard_map/all_to_all | solution.py:31
  82.2 0.3 reduce_sum.9
  82.5 0.0 copy-done.6
  82.6 0.0 copy-done.7
  82.6 0.0 copy-done.8
  82.6 0.0 copy-done.9
  82.6 0.6 convert_bitcast_fusion.1
  83.2 0.1 copy.64
  83.3 0.1 copy.65
  83.4 117.8 %reduce-scatter.2.cloned.1.call-done = f32[256,128]{1,0:T(8,128)} async-done(((f32[16384,128]{1,0:T(8,128)}), f32[256,128]{1,0:T(8,128)}) %reduce-scatter.2.cloned.1.call-update) | async-done | bytes 131088 | tf_op jit(solution)/shard_map/reduce_scatter | solution.py:21
  201.2 0.9 multiply_multiply_fusion
  202.1 0.2 mul.127
  202.3 0.2 copy.62
  202.5 0.2 mul.133
  202.7 0.2 copy.61
  202.9 0.0 copy-done
  202.9 0.0 copy-done.1
  202.9 0.7 fusion
  203.5 0.0 copy-done.2
  203.5 0.0 copy-done.3
  203.5 0.7 convert_bitcast_fusion
  204.2 0.1 concatenate.11
  204.3 0.3 stack.2
  204.6 115.4 %all_to_all.11 = bf16[64,16,2050]{2,1,0:T(8,128)(2,1)S(1)} all-to-all(bf16[64,16,2050]{2,1,0:T(8,128)(2,1)S(1)} %stack.2), channel_id=1, replica_groups=mesh['replica'=64,'model'=4] {'replica'}, dimensions={0} | all-to-all | bytes 8396800 | tf_op jit(solution)/shard_map/all_to_all | solution.py:54
  320.0 1.9 slice_bitcast_fusion
  321.9 0.9 slice_reduce_fusion
  322.8 2.5 copy.66
  (4 shorter events, 0.0 us)
Async XLA Ops:
  7.2 194.0 %reduce-scatter.2.cloned.1.call-start = ((), (), s32[]{:S(2)}) async-start(), calls=%async_computation.3 | async-start | bytes 8519680 | tf_op jit(solution)/shard_map/reduce_scatter | solution.py:21
  49.6 0.7 copy-start.4
  49.6 0.7 copy-start.5
  49.6 32.9 %copy-start.6 = (f32[16]{0:T(128)S(1)}, f32[16]{0:T(128)}, u32[]{:S(2)}) copy-start(f32[16]{0:T(128)} %param.19) | copy-start | bytes 196
  49.6 32.9 %copy-start.7 = (f32[16]{0:T(128)S(1)}, f32[16]{0:T(128)}, u32[]{:S(2)}) copy-start(f32[16]{0:T(128)} %param.23) | copy-start | bytes 196
  49.6 32.9 %copy-start.8 = (f32[16]{0:T(128)S(1)}, f32[16]{0:T(128)}, u32[]{:S(2)}) copy-start(f32[16]{0:T(128)} %param.18) | copy-start | bytes 196
  49.6 32.9 %copy-start.9 = (f32[16]{0:T(128)S(1)}, f32[16]{0:T(128)}, u32[]{:S(2)}) copy-start(f32[16]{0:T(128)} %param.22) | copy-start | bytes 196
  49.7 153.2 %copy-start = (f32[16,1024]{1,0:T(8,128)S(1)}, f32[16,1024]{1,0:T(8,128)}, u32[]{:S(2)}) copy-start(f32[16,1024]{1,0:T(8,128)} %param.16) | copy-start | bytes 196612
  49.7 153.2 %copy-start.1 = (f32[16,1024]{1,0:T(8,128)S(1)}, f32[16,1024]{1,0:T(8,128)}, u32[]{:S(2)}) copy-start(f32[16,1024]{1,0:T(8,128)} %param.20) | copy-start | bytes 196612
  49.7 153.8 %copy-start.2 = (f32[1024,16]{0,1:T(8,128)S(1)}, f32[1024,16]{0,1:T(8,128)}, u32[]{:S(2)}) copy-start(f32[1024,16]{0,1:T(8,128)} %param.17) | copy-start | bytes 196612
  49.7 153.8 %copy-start.3 = (f32[1024,16]{0,1:T(8,128)S(1)}, f32[1024,16]{0,1:T(8,128)}, u32[]{:S(2)}) copy-start(f32[1024,16]{0,1:T(8,128)} %param.21) | copy-start | bytes 196612
  51.4 30.8 %all-to-all-start = ((f32[64,1,2048]{2,1,0:T(1,128)}), f32[64,1,2048]{2,1,0:T(1,128)S(1)}, u32[]{:S(2)}, u32[]{:S(2)}) async-start(f32[64,1,2048]{2,1,0:T(1,128)} %broadcast_in_dim.2), calls=%async_computation.1 | async-start | bytes 1048576 | tf_op jit(solution)/shard_map/all_to_all | solution.py:31
Sparse Core Ops, SparseCore 0:
  49.8 151.3 reduce-scatter.1
